TPU v7x, 32 devices: a whole 2x2x4 slice. The times are simulated.
32 devices in a mesh: grp: 2 (over y), bn: 16 (over z, x, core).
Axes of the slice: x: 2, y: 2, z: 4, core: 2. Of those that a mesh axis runs over, the one named last changes fastest.
Arguments:
- images: bfloat16 [32, 19, 19, 384], P(('grp', 'bn')), parts along dimension 0, may hold values from -56 to 56
- expand_weight: bfloat16 [384, 2304], P('bn'), may hold values from -0.3125 to 0.3125
- expand_gain: float32 [2304], replicated, may hold values from 0.5 to 2
- expand_shift: float32 [2304], replicated, may hold values from -3 to 3
- depth_weight: bfloat16 [25, 2304], replicated, may hold values from -1.25 to 1.25
- depth_gain: float32 [2304], replicated, may hold values from 0.5 to 2
- depth_shift: float32 [2304], replicated, may hold values from -3 to 3
- squeeze_weight: bfloat16 [2304, 96], replicated, may hold values from -0.125 to 0.125
- squeeze_bias: float32 [96], replicated, may hold values from -4 to 4
- excite_weight: bfloat16 [96, 2304], replicated, may hold values from -0.625 to 0.625
- excite_bias: float32 [2304], replicated, may hold values from -4 to 4
- project_weight: bfloat16 [2304, 384], P('bn'), may hold values from -0.125 to 0.125
- project_gain: float32 [384], replicated, may hold values from 0.5 to 2
- project_shift: float32 [384], replicated, may hold values from -3 to 3
- group_table: int32 [32], P('grp'), parts along dimension 0, may hold values from 0 to 1, as said below
Outputs:
- block_output: bfloat16 [32, 19, 19, 384], P(('grp', 'bn')), parts along dimension 0
There are 2 independent parts, one for each index of `grp`. A program takes and returns all parts, laid end to end along the dimension named above; an argument that names none is the same for every part. Nothing has to cross between parts.
Inputs may be any that keep to these rules, and one draw needn't show every extreme that they name: `group_table`: each of the 2 statistics groups holds at least 4 images, placed anywhere among the images.
All inputs are finite; a program needn't handle non-finite values.
Results may differ from a plain program's by a relative error of at most 0.0065.
Values may be sent and summed in bfloat16 or wider, within the bound.
A program may use at most 64 MiB of HBM per device.

v0:
```python
import jax
import jax.numpy as jnp
from jax import lax
from jax.sharding import PartitionSpec as P

KERNEL = 5
STAT_GROUPS = 2
epsilon = 0.001


def normalize(values, centre, inverse, gain, shift):
    return (values.astype(jnp.float32) - centre) * inverse * gain + shift


def depthwise(widened, depth_weight, height, breadth):
    spatial = widened.reshape(height, breadth, widened.shape[-1])
    margin = KERNEL // 2
    padded = jnp.pad(spatial, ((margin, margin), (margin, margin), (0, 0)))
    accumulated = jnp.zeros(spatial.shape, jnp.float32)
    for row_shift in range(KERNEL):
        for col_shift in range(KERNEL):
            window = padded[row_shift : row_shift + height, col_shift : col_shift + breadth]
            accumulated = accumulated + window.astype(jnp.float32) * depth_weight[
                row_shift * KERNEL + col_shift
            ].astype(jnp.float32)
    return accumulated.reshape(height * breadth, spatial.shape[-1]).astype(jnp.bfloat16)


def group_moments(values, selector, population):
    totals = jnp.sum(values, axis=0, dtype=jnp.float32)
    squares = jnp.sum(jnp.square(values.astype(jnp.float32)), axis=0)
    weighted = selector[:, None, None] * jnp.stack([totals, squares])[None]
    summed = lax.psum(weighted, "bn")
    picked = jnp.sum(selector[:, None, None] * summed, axis=0)
    centre = picked[0] / population
    spread = picked[1] / population - centre * centre
    return (centre, lax.rsqrt(spread + epsilon))


def on_device(
    images,
    expand_weight,
    expand_gain,
    expand_shift,
    depth_weight,
    depth_gain,
    depth_shift,
    squeeze_weight,
    squeeze_bias,
    excite_weight,
    excite_bias,
    project_weight,
    project_gain,
    project_shift,
    group_table,
):
    height, breadth, channels = (images.shape[1], images.shape[2], images.shape[3])
    pixels = height * breadth
    flattened = images.reshape(pixels, channels)
    device_rank = lax.axis_index("bn")
    ranks_all = jnp.arange(group_table.shape[0], dtype=jnp.int32)
    my_group = jnp.sum(jnp.where(ranks_all == device_rank, group_table, 0))
    members = jnp.sum((group_table == my_group).astype(jnp.float32))
    population = members * pixels
    selector = (jnp.arange(STAT_GROUPS, dtype=jnp.int32) == my_group).astype(jnp.float32)
    inputs = flattened
    expanded = jnp.dot(
        inputs,
        lax.all_gather(expand_weight, "bn", axis=0, tiled=True),
        preferred_element_type=jnp.float32,
    ).astype(jnp.bfloat16)
    centre, inverse = group_moments(expanded, selector, population)
    widened = jax.nn.silu(normalize(expanded, centre, inverse, expand_gain, expand_shift)).astype(
        jnp.bfloat16
    )
    filtered = depthwise(widened, depth_weight, height, breadth)
    centre, inverse = group_moments(filtered, selector, population)
    activated = jax.nn.silu(normalize(filtered, centre, inverse, depth_gain, depth_shift)).astype(
        jnp.bfloat16
    )
    pooled = (jnp.sum(activated, axis=0, dtype=jnp.float32) / pixels).astype(jnp.bfloat16)[None, :]
    squeezed = jax.nn.silu(
        jnp.dot(pooled, squeeze_weight, preferred_element_type=jnp.float32) + squeeze_bias
    ).astype(jnp.bfloat16)
    excitation = jax.nn.sigmoid(
        jnp.dot(squeezed, excite_weight, preferred_element_type=jnp.float32) + excite_bias
    )
    gated_input = (activated * excitation).astype(jnp.bfloat16)
    inputs = gated_input
    projected = jnp.dot(
        inputs,
        lax.all_gather(project_weight, "bn", axis=0, tiled=True),
        preferred_element_type=jnp.float32,
    ).astype(jnp.bfloat16)
    centre, inverse = group_moments(projected, selector, population)
    output = flattened.astype(jnp.float32) + normalize(
        projected, centre, inverse, project_gain, project_shift
    )
    return output.astype(jnp.bfloat16).reshape(images.shape)


def solution(mesh):
    return jax.shard_map(
        on_device,
        mesh=mesh,
        in_specs=(
            P(("grp", "bn"), None, None, None),
            P("bn", None),
            P(),
            P(),
            P(),
            P(),
            P(),
            P(),
            P(),
            P(),
            P(),
            P("bn", None),
            P(),
            P(),
            P("grp"),
        ),
        out_specs=P(("grp", "bn"), None, None, None),
        check_vma=False,
    )
```

profile of v0, /device:TPU:0, one launch (start us, length us, event | category | flops | bytes accessed | tf_op | source)
XLA Modules:
  0.0 257.8 jit_solution(15007953222312947867)
XLA Ops:
  6.5 0.0 copy-start
  6.5 0.0 all-gather.3.cloned.1.call-start
  6.5 0.7 all-gather.3.cloned.1.call-update
  7.3 0.0 all-gather.5.cloned.1.call-start
  7.3 0.7 all-gather.5.cloned.1.call-update
  8.0 1.3 fusion.15
  9.3 0.6 compare_convert_fusion.1
  10.0 1.9 fusion.16
  11.9 1.9 convert_reduce_fusion.27
  13.7 1.1 convert_reduce_fusion.26
  14.9 1.1 reshape.239
  16.5 0.0 copy-start.2
  16.5 0.0 copy-start.3
  16.6 36.0 %all-gather.3.cloned.1.call-done = bf16[384,2304]{1,0:T(8,128)(2,1)} async-done(((bf16[24,2304]{1,0:T(8,128)(2,1)}), bf16[384,2304]{1,0:T(8,128)(2,1)}) %all-gather.3.cloned.1.call-update) | async-done | bytes 1769488 | tf_op jit(solution)/shard_map/all_gather | solution.py:69
  52.5 3.7 %convert_reduce_fusion = (f32[2304]{0:T(1024)S(1)}, f32[2304]{0:T(1024)S(1)}, bf16[361,2304]{1,0:T(8,128)(2,1)}) fusion(bf16[361,384]{1,0:T(8,128)(2,1)S(1)} %reshape.239, bf16[384,2304]{1,0:T(8,128)(2,1)} %all-gather.3.cloned.1.call-done), kind=kOutput, calls=%fused_computation.2 | convolution fusion | flops 642933504 | bytes 3728640 | tf_op jit(solution)/shard_map/dot_general | solution.py:67
  56.3 0.1 broadcast_multiply_fusion.1
  56.4 59.8 %psum.21 = f32[2,2,2304]{2,1,0:T(2,128)S(1)} all-reduce(f32[2,2,2304]{2,1,0:T(2,128)S(1)} %broadcast_multiply_fusion.1), channel_id=1, replica_groups=mesh['grp'=2,'bn'=16] {'bn'}, use_global_device_ids=true, to_apply=%region_3.4 | all-reduce | flops 9216 | bytes 73728 | tf_op jit(solution)/shard_map/psum | solution.py:33
  116.2 0.1 multiply_reduce_fusion.3
  116.3 0.1 fusion.26
  116.3 0.0 copy-done.2
  116.4 0.0 copy-done.3
  116.4 2.6 %fusion.9 = bf16[361,2304]{1,0:T(8,128)(2,1)S(1)} fusion(bf16[361,2304]{1,0:T(8,128)(2,1)} %get-tuple-element.43, f32[2304]{0:T(1024)S(1)} %copy-done.2, f32[2304]{0:T(1024)S(1)} %copy-done.3, f32[2304]{0:T(1024)S(1)} %get-tuple-element.39, f32[2304]{0:T(1024)S(1)} %get-tuple-element.38), kind=kLoop, calls=%fused_computation.17 | loop fusion | flops 8317440 | bytes 3363840 | tf_op jit(solution)/shard_map/convert_element_type | solution.py:73
  119.0 2.0 reshape.240
  121.0 32.3 %convert_reduce_fusion.2 = (f32[2304]{0:T(1024)S(1)}, f32[2304]{0:T(1024)S(1)}, bf16[19,19,2304]{2,1,0:T(8,128)(2,1)S(1)}) fusion(f32[2304]{0:T(1024)S(1)} %get-tuple-element.34, f32[2304]{0:T(1024)S(1)} %get-tuple-element.35, f32[2304]{0:T(1024)S(1)} %get-tuple-element.12, f32[2304]{0:T(1024)S(1)} %get-tuple-element.13, f32[2304]{0:T(1024)S(1)} %get-tuple-element.14, ...), kind=kLoop, calls=%fused_computation.20 | loop fusion | flops 65703168 | bytes 3575808 | tf_op jit(solution)/shard_map/reduce_sum | solution.py:30
  153.3 0.0 copy-start.4
  153.3 0.0 copy-start.5
  153.3 0.0 copy-start.1
  153.3 0.0 copy-start.9
  153.4 0.0 copy-start.6
  153.4 2.2 reshape.267
  155.6 0.1 broadcast_multiply_fusion
  155.7 57.9 %psum.22 = f32[2,2,2304]{2,1,0:T(2,128)S(1)} all-reduce(f32[2,2,2304]{2,1,0:T(2,128)S(1)} %broadcast_multiply_fusion), channel_id=1, replica_groups=mesh['grp'=2,'bn'=16] {'bn'}, use_global_device_ids=true, to_apply=%region_8.9 | all-reduce | flops 9216 | bytes 73728 | tf_op jit(solution)/shard_map/psum | solution.py:33
  213.6 0.1 multiply_reduce_fusion.2
  213.7 0.1 fusion.25
  213.7 0.0 copy-done.4
  213.8 1.6 convert_reduce_fusion.1
  215.4 0.4 convolution_reduce_fusion
  215.8 0.0 copy-done.6
  215.8 0.0 copy-start.7
  215.8 0.0 copy-start.8
  215.9 0.0 all-gather.5.cloned.1.call-done
  215.9 3.9 %fusion.24 = (f32[384]{0:T(512)S(1)}, f32[384]{0:T(512)S(1)}, f32[361,384]{1,0:T(8,128)S(1)}) fusion(bf16[2304,384]{1,0:T(8,128)(2,1)} %all-gather.5.cloned.1.call-done, f32[2304]{0:T(1024)S(1)} %add_divide_fusion, f32[2304]{0:T(1024)S(1)} %copy-done.4, f32[2304]{0:T(1024)S(1)} %copy-done.5, f32[2304]{0:T(1024)S(1)} %get-tuple-element.37, ...), kind=kOutput, calls=%fused_computation.106 | convolution fusion | flops 649452672 | bytes 5700096 | tf_op jit(solution)/shard_map/dot_general | solution.py:90
  219.8 0.1 broadcast_multiply_fusion.2
  219.9 30.0 %psum.23 = f32[2,2,384]{2,1,0:T(2,128)S(1)} all-reduce(f32[2,2,384]{2,1,0:T(2,128)S(1)} %broadcast_multiply_fusion.2), channel_id=1, replica_groups=mesh['grp'=2,'bn'=16] {'bn'}, use_global_device_ids=true, to_apply=%region_13.14 | all-reduce | flops 1536 | bytes 12288 | tf_op jit(solution)/shard_map/psum | solution.py:33
  249.9 0.1 multiply_reduce_fusion.4
  250.0 0.0 copy-done.8
  250.0 0.1 add_convert_fusion.1
  250.2 0.8 reshape.241
  (18 shorter events, 0.2 us)
Async XLA Ops:
  6.5 208.8 %copy-start = (bf16[96,2304]{1,0:T(8,128)(2,1)S(1)}, bf16[96,2304]{1,0:T(8,128)(2,1)}, u32[]{:S(2)}) copy-start(bf16[96,2304]{1,0:T(8,128)(2,1)} %param.24) | copy-start | bytes 1327108
  6.5 46.0 %all-gather.3.cloned.1.call-start = ((), (), s32[]{:S(2)}) async-start(), calls=%async_computation | async-start | bytes 1880064 | tf_op jit(solution)/shard_map/all_gather | solution.py:69
  7.3 208.6 %all-gather.5.cloned.1.call-start = ((), (), s32[]{:S(2)}) async-start(), calls=%async_computation.1 | async-start | bytes 1880064 | tf_op jit(solution)/shard_map/all_gather | solution.py:92
  16.5 99.8 %copy-start.2 = (f32[2304]{0:T(1024)S(1)}, f32[2304]{0:T(1024)}, u32[]{:S(2)}) copy-start(f32[2304]{0:T(1024)} %param.18) | copy-start | bytes 27652
  16.5 99.8 %copy-start.3 = (f32[2304]{0:T(1024)S(1)}, f32[2304]{0:T(1024)}, u32[]{:S(2)}) copy-start(f32[2304]{0:T(1024)} %param.17) | copy-start | bytes 27652
  153.3 60.4 %copy-start.4 = (f32[2304]{0:T(1024)S(1)}, f32[2304]{0:T(1024)}, u32[]{:S(2)}) copy-start(f32[2304]{0:T(1024)} %param.21) | copy-start | bytes 27652
  153.3 60.4 %copy-start.5 = (f32[2304]{0:T(1024)S(1)}, f32[2304]{0:T(1024)}, u32[]{:S(2)}) copy-start(f32[2304]{0:T(1024)} %param.20) | copy-start | bytes 27652
  153.3 62.0 %copy-start.1 = (bf16[2304,96]{0,1:T(8,128)(2,1)S(1)}, bf16[2304,96]{0,1:T(8,128)(2,1)}, u32[]{:S(2)}) copy-start(bf16[2304,96]{0,1:T(8,128)(2,1)} %param.22) | copy-start | bytes 1327108
  153.3 62.0 %copy-start.9 = (f32[96]{0:T(128)S(1)}, f32[96]{0:T(128)}, u32[]{:S(2)}) copy-start(f32[96]{0:T(128)} %param.23) | copy-start | bytes 1156
  153.4 62.5 %copy-start.6 = (f32[2304]{0:T(1024)S(1)}, f32[2304]{0:T(1024)}, u32[]{:S(2)}) copy-start(f32[2304]{0:T(1024)} %param.25) | copy-start | bytes 27652
  215.8 34.2 %copy-start.7 = (f32[384]{0:T(512)S(1)}, f32[384]{0:T(512)}, u32[]{:S(2)}) copy-start(f32[384]{0:T(512)} %param.28) | copy-start | bytes 4612
  215.8 34.2 %copy-start.8 = (f32[384]{0:T(512)S(1)}, f32[384]{0:T(512)}, u32[]{:S(2)}) copy-start(f32[384]{0:T(512)} %param.27) | copy-start | bytes 4612
Sparse Core Ops, SparseCore 0:
  9.5 42.9 all-gather.2
  54.7 39.2 all-gather.4
where the time goes:
time: 258 us
  blocking collectives  148 us (57%)
  other arithmetic  44.2 us (17%)
  waiting for transfers between devices  37.4 us (14%)
  between operations  14.3 us (6%)
  matrix products  8.06 us (3%)
  local copies, waits for them, and re-layouts  6.24 us (2%)
    psum x3, blocking collectives, group_moments(): summed = lax.psum(weighted, 'bn')  148 us
    all_gather x1, waiting for transfers between devices, on_device(): lax.all_gather(expand_weight, 'bn', axis=0, tiled=True)  36 us
    reduce_sum x1, other arithmetic, group_moments(): totals = jnp.sum(values, axis=0, dtype=jnp.float32)  32.3 us
  transfers between devices with their start and end apart: 2, of which 1 were waited for; matrix products, arithmetic and copies ran while one was open for 21% of the time, Pallas kernels for 0%

commit v1 on v0

--- a/solution.py
+++ b/solution.py
@@ -6,6 +6,13 @@
 KERNEL = 5
 STAT_GROUPS = 2
 epsilon = 0.001
+
+
+def exchange_gather(block, mesh_axis, d):
+    devices = lax.axis_size(mesh_axis)
+    blocks = jnp.stack([block for _ in range(devices)])
+    blocks = lax.all_to_all(blocks, mesh_axis, split_axis=0, concat_axis=0)
+    return jnp.concatenate(blocks, axis=d)
 
 
 def normalize(values, centre, inverse, gain, shift):
@@ -65,9 +72,7 @@
     selector = (jnp.arange(STAT_GROUPS, dtype=jnp.int32) == my_group).astype(jnp.float32)
     inputs = flattened
     expanded = jnp.dot(
-        inputs,
-        lax.all_gather(expand_weight, "bn", axis=0, tiled=True),
-        preferred_element_type=jnp.float32,
+        inputs, exchange_gather(expand_weight, "bn", 0), preferred_element_type=jnp.float32
     ).astype(jnp.bfloat16)
     centre, inverse = group_moments(expanded, selector, population)
     widened = jax.nn.silu(normalize(expanded, centre, inverse, expand_gain, expand_shift)).astype(

time: 258 us -> 270 us (1.047)
  blocking collectives: 148 us -> 158 us
  starting transfers between devices: 0.04 us -> 7.43 us
  other arithmetic: 44.2 us -> 41.2 us
    all_gather x1 -> x0, waiting for transfers between devices: 36 us -> none  [on_device(): lax.all_gather(expand_weight, 'bn', axis=0, tiled=True)]
    all_to_all x0 -> x1, waiting for transfers between devices: none -> 34.1 us  [exchange_gather(): blocks = lax.all_to_all(blocks, mesh_axis, split_axis=0, concat_axis=0)]
    psum x3, blocking collectives: 148 us -> 158 us  [group_moments(): summed = lax.psum(weighted, 'bn')]
    all_to_all x0 -> x1, starting transfers between devices: none -> 7.39 us  [exchange_gather(): blocks = lax.all_to_all(blocks, mesh_axis, split_axis=0, concat_axis=0)]
  transfers between devices with their start and end apart: 2 -> 2, of which waited for: 1 -> 1; matrix products, arithmetic and copies ran while one was open for 21% -> 18% of each run, Pallas kernels for 0% -> 0%
where the time goes in v1:
time: 270 us
  blocking collectives  158 us (59%)
  other arithmetic  41.2 us (15%)
  waiting for transfers between devices  34.8 us (13%)
  between operations  14.4 us (5%)
  local copies, waits for them, and re-layouts  7.53 us (3%)
  starting transfers between devices  7.43 us (3%)
  matrix products  6.58 us (2%)
    psum x3, blocking collectives, group_moments(): summed = lax.psum(weighted, 'bn')  158 us
    all_to_all x1, waiting for transfers between devices, exchange_gather(): blocks = lax.all_to_all(blocks, mesh_axis, split_axis=0, concat_axis=0)  34.1 us
    reduce_sum x1, other arithmetic, group_moments(): totals = jnp.sum(values, axis=0, dtype=jnp.float32)  33 us
    all_to_all x1, starting transfers between devices, exchange_gather(): blocks = lax.all_to_all(blocks, mesh_axis, split_axis=0, concat_axis=0)  7.39 us
  transfers between devices with their start and end apart: 2, of which 1 were waited for; matrix products, arithmetic and copies ran while one was open for 18% of the time, Pallas kernels for 0%

profile of v1, /device:TPU:0, one launch (start us, length us, event | category | flops | bytes accessed | tf_op | source)
XLA Modules:
  0.0 269.6 jit_solution(13897279232707616513)
XLA Ops:
  6.5 0.0 copy-start
  6.5 2.3 stack.20
  8.9 7.4 %all-to-all-start = ((bf16[16,24,2304]{2,1,0:T(8,128)(2,1)}), bf16[16,24,2304]{2,1,0:T(8,128)(2,1)S(1)}, u32[]{:S(2)}, u32[]{:S(2)}) async-start(bf16[16,24,2304]{2,1,0:T(8,128)(2,1)} %stack.20), calls=%async_computation | async-start | bytes 3538944 | tf_op jit(solution)/shard_map/all_to_all | solution.py:14
  16.2 0.0 all-gather.2.cloned.1.call-start
  16.3 0.7 all-gather.2.cloned.1.call-update
  17.0 0.0 copy-done.3
  17.0 0.1 reshape.244
  17.1 0.0 copy-done.12
  17.1 0.6 fusion.15
  17.8 1.3 fusion.16
  19.7 0.7 compare_convert_fusion.1
  20.3 0.0 copy-done.2
  20.3 0.2 convert_reduce_fusion.26
  20.5 0.5 convert_reduce_fusion.27
  21.0 34.1 %all-to-all-done = bf16[16,24,2304]{2,1,0:T(8,128)(2,1)S(1)} async-done(((bf16[16,24,2304]{2,1,0:T(8,128)(2,1)}), bf16[16,24,2304]{2,1,0:T(8,128)(2,1)S(1)}, u32[]{:S(2)}, u32[]{:S(2)}) %all-to-all-start) | async-done | bytes 1769504 | tf_op jit(solution)/shard_map/all_to_all | solution.py:14
  55.1 2.3 convert_reduce_fusion
  57.4 0.1 broadcast_multiply_fusion.1
  57.5 69.8 %psum.21 = f32[2,2,2304]{2,1,0:T(2,128)S(1)} all-reduce(f32[2,2,2304]{2,1,0:T(2,128)S(1)} %broadcast_multiply_fusion.1), channel_id=1, replica_groups=mesh['grp'=2,'bn'=16] {'bn'}, use_global_device_ids=true, to_apply=%region_3.4 | all-reduce | flops 9216 | bytes 73728 | tf_op jit(solution)/shard_map/psum | solution.py:40
  127.3 0.1 multiply_reduce_fusion.3
  127.4 0.1 fusion.26
  127.5 0.0 copy-done.4
  127.5 0.0 copy-done.5
  127.5 2.6 fusion.9
  130.1 2.0 reshape.246
  132.1 33.0 %convert_reduce_fusion.2 = (f32[2304]{0:T(1024)S(1)}, f32[2304]{0:T(1024)S(1)}, bf16[19,19,2304]{2,1,0:T(8,128)(2,1)S(1)}) fusion(f32[2304]{0:T(1024)S(1)} %get-tuple-element.34, f32[2304]{0:T(1024)S(1)} %get-tuple-element.35, f32[2304]{0:T(1024)S(1)} %get-tuple-element.12, f32[2304]{0:T(1024)S(1)} %get-tuple-element.13, f32[2304]{0:T(1024)S(1)} %get-tuple-element.14, ...), kind=kLoop, calls=%fused_computation.20 | loop fusion | flops 65703168 | bytes 3575808 | tf_op jit(solution)/shard_map/reduce_sum | solution.py:37
  165.1 0.0 copy-start.6
  165.1 0.0 copy-start.7
  165.1 0.0 copy-start.1
  165.1 0.0 copy-start.11
  165.1 0.0 copy-start.8
  165.2 2.2 reshape.273
  167.4 0.1 broadcast_multiply_fusion
  167.5 57.9 %psum.22 = f32[2,2,2304]{2,1,0:T(2,128)S(1)} all-reduce(f32[2,2,2304]{2,1,0:T(2,128)S(1)} %broadcast_multiply_fusion), channel_id=1, replica_groups=mesh['grp'=2,'bn'=16] {'bn'}, use_global_device_ids=true, to_apply=%region_8.9 | all-reduce | flops 9216 | bytes 73728 | tf_op jit(solution)/shard_map/psum | solution.py:40
  225.3 0.1 multiply_reduce_fusion.2
  225.4 0.1 fusion.25
  225.5 0.0 copy-done.6
  225.5 0.0 copy-done.7
  225.5 1.6 convert_reduce_fusion.1
  227.1 0.4 convolution_reduce_fusion
  227.6 0.0 copy-start.9
  227.6 0.0 copy-start.10
  227.6 0.0 all-gather.2.cloned.1.call-done
  227.6 3.9 %fusion.24 = (f32[384]{0:T(512)S(1)}, f32[384]{0:T(512)S(1)}, f32[361,384]{1,0:T(8,128)S(1)}) fusion(bf16[2304,384]{1,0:T(8,128)(2,1)} %all-gather.2.cloned.1.call-done, f32[2304]{0:T(1024)S(1)} %add_divide_fusion, f32[2304]{0:T(1024)S(1)} %copy-done.6, f32[2304]{0:T(1024)S(1)} %copy-done.7, f32[2304]{0:T(1024)S(1)} %get-tuple-element.37, ...), kind=kOutput, calls=%fused_computation.106 | convolution fusion | flops 649452672 | bytes 5700096 | tf_op jit(solution)/shard_map/dot_general | solution.py:95
  231.6 0.1 broadcast_multiply_fusion.2
  231.7 30.0 %psum.23 = f32[2,2,384]{2,1,0:T(2,128)S(1)} all-reduce(f32[2,2,384]{2,1,0:T(2,128)S(1)} %broadcast_multiply_fusion.2), channel_id=1, replica_groups=mesh['grp'=2,'bn'=16] {'bn'}, use_global_device_ids=true, to_apply=%region_13.14 | all-reduce | flops 1536 | bytes 12288 | tf_op jit(solution)/shard_map/psum | solution.py:40
  261.6 0.1 multiply_reduce_fusion.4
  261.8 0.1 add_convert_fusion.1
  261.9 0.8 reshape.247
  (24 shorter events, 0.2 us)
Async XLA Ops:
  6.5 220.6 %copy-start = (bf16[96,2304]{1,0:T(8,128)(2,1)S(1)}, bf16[96,2304]{1,0:T(8,128)(2,1)}, u32[]{:S(2)}) copy-start(bf16[96,2304]{1,0:T(8,128)(2,1)} %param.24) | copy-start | bytes 1327108
  6.5 10.5 %copy-start.3 = (bf16[1,19,19,384]{3,2,1,0:T(8,128)(2,1)S(1)}, bf16[1,19,19,384]{3,2,1,0:T(8,128)(2,1)}, u32[]{:S(2)}) copy-start(bf16[1,19,19,384]{3,2,1,0:T(8,128)(2,1)} %param.15) | copy-start | bytes 831748
  6.5 10.6 %copy-start.12 = (s32[16]{0:T(128)S(1)}, s32[16]{0:T(128)}, u32[]{:S(2)}) copy-start(s32[16]{0:T(128)} %param.29) | copy-start | bytes 196
  6.5 13.8 %copy-start.2 = (bf16[25,2304]{1,0:T(8,128)(2,1)S(1)}, bf16[25,2304]{1,0:T(8,128)(2,1)}, u32[]{:S(2)}) copy-start(bf16[25,2304]{1,0:T(8,128)(2,1)} %param.19) | copy-start | bytes 345604
  8.9 46.2 %all-to-all-start = ((bf16[16,24,2304]{2,1,0:T(8,128)(2,1)}), bf16[16,24,2304]{2,1,0:T(8,128)(2,1)S(1)}, u32[]{:S(2)}, u32[]{:S(2)}) async-start(bf16[16,24,2304]{2,1,0:T(8,128)(2,1)} %stack.20), calls=%async_computation | async-start | bytes 3538944 | tf_op jit(solution)/shard_map/all_to_all | solution.py:14
  16.2 211.4 %all-gather.2.cloned.1.call-start = ((), (), s32[]{:S(2)}) async-start(), calls=%async_computation.1 | async-start | bytes 1880064 | tf_op jit(solution)/shard_map/all_gather | solution.py:97
  55.1 72.4 %copy-start.4 = (f32[2304]{0:T(1024)S(1)}, f32[2304]{0:T(1024)}, u32[]{:S(2)}) copy-start(f32[2304]{0:T(1024)} %param.18) | copy-start | bytes 27652
  55.1 72.4 %copy-start.5 = (f32[2304]{0:T(1024)S(1)}, f32[2304]{0:T(1024)}, u32[]{:S(2)}) copy-start(f32[2304]{0:T(1024)} %param.17) | copy-start | bytes 27652
  165.1 60.4 %copy-start.6 = (f32[2304]{0:T(1024)S(1)}, f32[2304]{0:T(1024)}, u32[]{:S(2)}) copy-start(f32[2304]{0:T(1024)} %param.21) | copy-start | bytes 27652
  165.1 60.4 %copy-start.7 = (f32[2304]{0:T(1024)S(1)}, f32[2304]{0:T(1024)}, u32[]{:S(2)}) copy-start(f32[2304]{0:T(1024)} %param.20) | copy-start | bytes 27652
  165.1 62.0 %copy-start.1 = (bf16[2304,96]{0,1:T(8,128)(2,1)S(1)}, bf16[2304,96]{0,1:T(8,128)(2,1)}, u32[]{:S(2)}) copy-start(bf16[2304,96]{0,1:T(8,128)(2,1)} %param.22) | copy-start | bytes 1327108
  165.1 62.0 %copy-start.11 = (f32[96]{0:T(128)S(1)}, f32[96]{0:T(128)}, u32[]{:S(2)}) copy-start(f32[96]{0:T(128)} %param.23) | copy-start | bytes 1156
  165.1 62.4 %copy-start.8 = (f32[2304]{0:T(1024)S(1)}, f32[2304]{0:T(1024)}, u32[]{:S(2)}) copy-start(f32[2304]{0:T(1024)} %param.25) | copy-start | bytes 27652
  227.6 34.2 %copy-start.9 = (f32[384]{0:T(512)S(1)}, f32[384]{0:T(512)}, u32[]{:S(2)}) copy-start(f32[384]{0:T(512)} %param.28) | copy-start | bytes 4612
  227.6 34.2 %copy-start.10 = (f32[384]{0:T(512)S(1)}, f32[384]{0:T(512)}, u32[]{:S(2)}) copy-start(f32[384]{0:T(512)} %param.27) | copy-start | bytes 4612
Sparse Core Ops, SparseCore 0:
  19.2 52.9 all-gather.1
